TPU v7x, 32 devices: a whole 2x2x4 slice. The times are simulated.
32 devices in a mesh: groups: 2 (over y), az: 4 (over z), rg: 2 (over x), acq: 2 (over core).
Axes of the slice: x: 2, y: 2, z: 4, core: 2. Of those that a mesh axis runs over, the one named last changes fastest.
Arguments:
- image_stack: bfloat16 [2, 64, 32, 4, 256], P(None, ('az', 'acq'), 'groups', 'rg'), parts along dimension 2, may hold values from -12 to 12
- steering: bfloat16 [4, 2, 64, 512], P('rg'), as said below
- wiener_filter: bfloat16 [4, 2, 64, 64], P('rg'), may hold values from -0.5 to 0.5
- range_group: int32 [4], P('rg'), may hold values from 0 to 3, as said below
- lay_list: int32 [32, 4, 32], P(('groups', 'az', 'acq'), 'rg'), parts along dimension 0, may hold values from 0 to 255, as said below
- lay_count: int32 [32, 4], P(('groups', 'az', 'acq'), 'rg'), parts along dimension 0, may hold values from 0 to 32, as said below
Outputs:
- power: bfloat16 [32, 4, 512, 256], P(('groups', 'az', 'acq'), 'rg'), parts along dimension 0
There are 2 independent parts, one for each index of `groups`. A program takes and returns all parts, laid end to end along the dimension named above; an argument that names none is the same for every part. Nothing has to cross between parts.
Inputs may be any that keep to these rules, and one draw needn't show every extreme that they name: `lay_list`: within one block the 32 entries are distinct pixels. The first lay_count entries of a block's list are its layover pixels; some block has 32. `range_group`: range block r belongs to a group from (r // 2) * 2 to (r // 2) * 2 + 1. `steering`: every complex entry has modulus 1 / sqrt(512) up to rounding.
All inputs are finite; a program needn't handle non-finite values.
Results may differ from a plain program's by a relative error of at most 0.0075.
Values may be sent and summed in bfloat16 or wider, within the bound.
No kernel may reach another device: no remote copies, remote signals or barrier semaphores. Data moves between devices by JAX's collectives and lax.ppermute only.
A program may use at most 64 MiB of HBM per device.

v0:
```python
import jax
import jax.numpy as jnp
from jax import lax
from jax.sharding import PartitionSpec as P

K = 64
E = 512
LMAX = 32
GRP_DEV = 2
ITERS = 8
STEP_SIZE = 0.5
SHRINK = 0.25
block_rows = 32


def complex_block(complex_parts):
    real_part = complex_parts[0]
    imag_part = complex_parts[1]
    upper = jnp.concatenate([real_part, -imag_part], axis=1)
    lower = jnp.concatenate([imag_part, real_part], axis=1)
    return jnp.concatenate([upper, lower], axis=0)


def ista_power(lane_data, operator):
    target = lane_data.astype(jnp.float32)
    elevation = operator.shape[1] // 2

    def sweep(sweep_index, estimate):
        rounded = estimate.astype(jnp.bfloat16)
        predicted = jnp.dot(rounded, operator.T, preferred_element_type=jnp.float32)
        misfit = (target - predicted).astype(jnp.bfloat16)
        update = estimate + STEP_SIZE * jnp.dot(
            misfit, operator, preferred_element_type=jnp.float32
        )
        magnitude = update[:, :elevation] ** 2 + update[:, elevation:] ** 2
        factor = jnp.maximum(1.0 - SHRINK * lax.rsqrt(jnp.maximum(magnitude, SHRINK * SHRINK)), 0.0)
        return update * jnp.concatenate([factor, factor], axis=1)

    start = jnp.zeros((lane_data.shape[0], 2 * elevation), jnp.float32)
    estimate = lax.fori_loop(0, ITERS, sweep, start)
    return (estimate[:, :elevation] ** 2 + estimate[:, elevation:] ** 2).astype(jnp.bfloat16)


def pack_order(usable):
    live_flags = usable.astype(jnp.int32)
    live_total = jnp.sum(live_flags)
    before_live = jnp.cumsum(live_flags) - live_flags
    before_empty = jnp.cumsum(1 - live_flags) - (1 - live_flags)
    lane_slot = jnp.where(usable, before_live, live_total + before_empty)
    source = (
        jnp.zeros_like(lane_slot).at[lane_slot].set(jnp.arange(lane_slot.shape[0], dtype=jnp.int32))
    )
    return (lane_slot, source, live_total)


def solve_lanes(lane_data, usable, operator):
    lane_slot, source, live_total = pack_order(usable)
    packed = jnp.take(lane_data, source, axis=0)
    lane_total = lane_data.shape[0]
    elevation = operator.shape[1] // 2

    def one_block(block_turn, result):
        row_block = lax.dynamic_slice_in_dim(packed, block_turn * block_rows, block_rows, 0)
        return lax.dynamic_update_slice_in_dim(
            result, ista_power(row_block, operator), block_turn * block_rows, 0
        )

    turns = (live_total + block_rows - 1) // block_rows
    result = lax.fori_loop(0, turns, one_block, jnp.zeros((lane_total, elevation), jnp.bfloat16))
    return jnp.take(result, lane_slot, axis=0)


def shards(image_stack, steering, wiener_filter, range_group, lay_list, lay_count):
    halves, acq_share, azb_all, range_local, block_pixels = image_stack.shape
    relaid = lax.all_to_all(
        image_stack.reshape(halves, 1, acq_share, azb_all, range_local, block_pixels),
        ("az", "acq"),
        split_axis=3,
        concat_axis=1,
        tiled=True,
    )
    blocks = lay_list.shape[0]
    pixels = relaid.reshape(2 * K, blocks, range_local, block_pixels)
    first_group = lax.axis_index("rg") * GRP_DEV
    operators = []
    wiener_sets = []
    lane_sets = []
    usable_sets = []
    chosen_sets = []
    for column in range(range_local):
        pick_group = jnp.arange(GRP_DEV, dtype=jnp.int32) == range_group[column] - first_group
        steer_parts = jnp.sum(
            jnp.where(pick_group[:, None, None, None], steering, jnp.zeros_like(steering)), axis=0
        )
        filter_parts = jnp.sum(
            jnp.where(
                pick_group[:, None, None, None], wiener_filter, jnp.zeros_like(wiener_filter)
            ),
            axis=0,
        )
        operator = complex_block(steer_parts)
        filter_matrix = complex_block(filter_parts)
        block_data = pixels[:, :, column, :]
        filtered = jnp.einsum(
            "ij,jap->iap", filter_matrix, block_data, preferred_element_type=jnp.float32
        ).astype(jnp.bfloat16)
        beamed = jnp.einsum("ie,iap->aep", operator, filtered, preferred_element_type=jnp.float32)
        wiener_sets.append(beamed[:, :E] ** 2 + beamed[:, E:] ** 2)
        listed = lay_list[:, column, :]
        live_count = lay_count[:, column]
        usable = jnp.arange(LMAX, dtype=jnp.int32)[None, :] < live_count[:, None]
        chosen = (
            (listed[:, :, None] == jnp.arange(block_pixels, dtype=jnp.int32)[None, None, :])
            & usable[:, :, None]
        ).astype(jnp.bfloat16)
        lane_data = jnp.einsum(
            "alp,iap->ali", chosen, block_data, preferred_element_type=jnp.float32
        ).astype(jnp.bfloat16)
        operators.append(operator)
        lane_sets.append(lane_data.reshape(blocks * LMAX, 2 * K))
        usable_sets.append(usable.reshape(blocks * LMAX))
        chosen_sets.append(chosen)
    powers = [
        solve_lanes(lane_sets[column], usable_sets[column], operators[column])
        for column in range(range_local)
    ]
    outputs = []
    for column in range(range_local):
        lay_power = powers[column].reshape(blocks, LMAX, E)
        placed = jnp.einsum(
            "alp,ale->aep", chosen_sets[column], lay_power, preferred_element_type=jnp.float32
        )
        covered = jnp.sum(chosen_sets[column].astype(jnp.float32), axis=1)
        outputs.append(
            jnp.where(covered[:, None, :] > 0.5, placed, wiener_sets[column]).astype(jnp.bfloat16)
        )
    return jnp.stack(outputs, axis=1)


def solution(mesh):
    return jax.shard_map(
        shards,
        mesh=mesh,
        in_specs=(
            P(None, ("az", "acq"), "groups", "rg", None),
            P("rg", None, None, None),
            P("rg", None, None, None),
            P("rg"),
            P(("groups", "az", "acq"), "rg", None),
            P(("groups", "az", "acq"), "rg"),
        ),
        out_specs=P(("groups", "az", "acq"), "rg", None, None),
        check_vma=False,
    )
```

profile of v0, /device:TPU:27, one launch (start us, length us, event | category | flops | bytes accessed | tf_op | source)
XLA Modules:
  0.0 42.8 jit_solution(8267527143187497523)
XLA Ops:
  0.0 1.9 %copy.39 = bf16[2,8,16,2,256]{4,3,1,0,2:T(2,128)(2,1)} copy(bf16[2,8,16,2,256]{4,3,2,1,0:T(2,128)(2,1)} %param.18) | data formatting | bytes 524288 | tf_op args[0]
  1.9 5.4 %all-to-all-start = ((bf16[2,1,8,16,2,256]{5,4,2,0,1,3:T(2,128)(2,1)}), bf16[2,1,8,16,2,256]{5,4,2,0,1,3:T(2,128)(2,1)S(1)}, u32[]{:S(2)}, u32[]{:S(2)}) async-start(bf16[2,1,8,16,2,256]{5,4,2,0,1,3:T(2,128)(2,1)} %bitcast.76), calls=%async_computation | async-start | bytes 524288 | tf_op jit(solution)/shard_map/all_to_all | solution.py:75
  7.3 1.0 %slice_reduce_fusion.1 = (s32[2]{0:T(128)S(1)}, s32[2]{0:T(128)S(1)}) fusion(s32[2,2]{1,0:T(2,128)} %param.23), kind=kLoop, calls=%fused_computation.142 | loop fusion | bytes 32 | tf_op jit(solution)/shard_map/slice | solution.py:110
  8.3 0.7 %convert_reduce_fusion.3 = s32[]{:T(128)} fusion(s32[2]{0:T(128)S(1)} %get-tuple-element.175), kind=kLoop, calls=%fused_computation.139 | loop fusion | flops 191 | bytes 12 | tf_op jit(solution)/shard_map/reduce_sum | solution.py:46
  9.4 0.8 %convert_reduce_fusion.2 = s32[]{:T(128)} fusion(s32[2]{0:T(128)S(1)} %get-tuple-element.176), kind=kLoop, calls=%fused_computation.136 | loop fusion | flops 191 | bytes 12 | tf_op jit(solution)/shard_map/reduce_sum | solution.py:46
  10.6 1.4 %fusion.92 = (s32[64]{0:T(128)S(1)}, s32[64]{0:T(128)S(1)}, s32[64]{0:T(128)S(1)}, s32[64]{0:T(128)S(1)}, s32[64]{0:T(128)S(1)}, /*index=5*/s32[64]{0:T(128)S(1)}) fusion(s32[64,1]{1,0:T(8,128)S(1)} %reduce-window.14, pred[64,1]{1,0:T(8,128)(4,1)S(1)} %lt.160, s32[64,1]{1,0:T(8,128)S(1)} %reduce-window.15, s32[]{:T(128)} %convert_reduce_fusion.3, ...), kind=kLoop, calls=%fused_computation.156 | loop fusion | flops 1152 | bytes 2696 | tf_op jit(solution)/shard_map/reduce-window
  12.0 0.8 %scatter_custom_fusion = s32[64]{0:T(128)S(1)} fusion(s32[64]{0:T(128)S(1)} %get-tuple-element.170, s32[64]{0:T(128)S(1)} %iota.35, s32[]{:T(128)} %constant.130.clone.1), kind=kCustom, calls=%fused_computation.148 | custom fusion | bytes 260 | tf_op jit(solution)/shard_map/scatter | solution.py:51
  12.8 1.3 %fusion.95 = (s32[1]{0:T(128)}, s32[1]{0:T(128)}) fusion(s32[2]{0:T(128)} %param.21), kind=kLoop, calls=%fused_computation.159 | loop fusion | bytes 16 | tf_op jit(solution)/shard_map/slice | solution.py:91
  15.5 1.1 %select_reduce_fusion.1 = (bf16[2,64,512]{2,1,0:T(8,128)(2,1)S(1)}, bf16[2,64,512]{2,1,0:T(8,128)(2,1)S(1)}) fusion(bf16[2,2,64,512]{3,2,1,0:T(8,128)(2,1)} %param.19, pred[2]{0:T(512)(128)(4,1)S(1)} %iota_compare_fusion.5, pred[2]{0:T(512)(128)(4,1)S(1)} %iota_compare_fusion.4), kind=kLoop, calls=%fused_computation.71 | loop fusion | flops 393216 | bytes 524292 | tf_op jit(solution)/shard_map/reduce_sum | solution.py:92
  16.7 0.8 %scatter_custom_fusion.1 = s32[64]{0:T(128)S(1)} fusion(s32[64]{0:T(128)S(1)} %get-tuple-element.230, s32[64]{0:T(128)S(1)} %iota.37, s32[]{:T(128)} %constant.130.clone.1), kind=kCustom, calls=%fused_computation.146 | custom fusion | bytes 260 | tf_op jit(solution)/shard_map/scatter | solution.py:51
  18.6 0.7 %compare_and_fusion = (pred[64]{0:T(512)(128)(4,1)S(1)}, s32[64]{0:T(128)S(1)}) fusion(pred[64]{0:T(512)(128)(4,1)S(1)} %lt.145, s32[64]{0:T(128)S(1)} %get-tuple-element.229, s32[]{:T(128)} %convert_reduce_fusion.2, s32[64]{0:T(128)S(1)} %get-tuple-element.231), kind=kLoop, calls=%fused_computation.132 | loop fusion | flops 768 | bytes 900 | tf_op jit(solution)/shard_map/jit(_take)/and | solution.py:70
  21.1 0.6 %gather_fusion = bf16[64,128]{1,0:T(8,128)(2,1)S(1)} fusion(bf16[64,128]{1,0:T(8,128)(2,1)S(1)} %bitcast.90, s32[1024]{0:T(1024)S(1)} %pad_clamp_fusion.3), kind=kCustom, calls=%fused_computation.clone | custom fusion | bytes 33024 | tf_op jit(solution)/shard_map/jit(_take)/gather | solution.py:58
  21.9 7.7 %while.47 = (s32[]{:T(128)}, bf16[64,512]{1,0:T(8,128)(2,1)S(1)}, s32[]{:T(128)}, bf16[64,128]{1,0:T(8,128)(2,1)S(1)}, bf16[128,1024]{1,0:T(8,128)(2,1)S(1)}, /*...) while((s32[]{:T(128)}, bf16[64,512]{1,0:T(8,128)(2,1)S(1)}, ...), condition=%wide.region_9.11_spmd, body=%wide.region_6.10_spmd.sunk | while | flops 17199112 | bytes 1253674 | solution.py:69
  21.9 3.8 %while.50 = (s32[]{:T(128)}, f32[32,1024]{1,0:T(8,128)S(1)}, bf16[128,1024]{1,0:T(8,128)(2,1)S(1)}, f32[32,128]{1,0:T(8,128)S(1)}, s32[]{:T(128)}, /*index=5*/s32[]{:T(128)}) while((s32[]{:T(128)}, f32[32,1024]{1,0:T(8,128)S(1)}, bf16[128,1024]{1,0:T(8,128)(2,1)S(1)}, f32[32,128]{1,0:T(8,128)S(1)}, s32[]{:T(128)}, ...), condition=%wide.region_8.9_spmd.clone, body=%wide.region_7.8_spmd.clone.sunk | while | flops 17129476 | bytes 1065039 | solution.py:40
  25.8 3.8 %while.50 = (s32[]{:T(128)}, f32[32,1024]{1,0:T(8,128)S(1)}, bf16[128,1024]{1,0:T(8,128)(2,1)S(1)}, f32[32,128]{1,0:T(8,128)S(1)}, s32[]{:T(128)}, /*index=5*/s32[]{:T(128)}) while((s32[]{:T(128)}, f32[32,1024]{1,0:T(8,128)S(1)}, bf16[128,1024]{1,0:T(8,128)(2,1)S(1)}, f32[32,128]{1,0:T(8,128)S(1)}, s32[]{:T(128)}, ...), condition=%wide.region_8.9_spmd.clone, body=%wide.region_7.8_spmd.clone.sunk | while | flops 17129476 | bytes 1065039 | solution.py:40
  29.6 0.6 %gather_fusion.2 = bf16[64,128]{1,0:T(8,128)(2,1)S(1)} fusion(bf16[64,128]{1,0:T(8,128)(2,1)S(1)} %bitcast.89, s32[1024]{0:T(1024)S(1)} %pad_clamp_fusion.1), kind=kCustom, calls=%fused_computation.2.clone | custom fusion | bytes 33024 | tf_op jit(solution)/shard_map/jit(_take)/gather | solution.py:58
  30.3 7.7 %while.49 = (s32[]{:T(128)}, bf16[64,512]{1,0:T(8,128)(2,1)S(1)}, s32[]{:T(128)}, bf16[64,128]{1,0:T(8,128)(2,1)S(1)}, bf16[128,1024]{1,0:T(8,128)(2,1)S(1)}, /*...) while((s32[]{:T(128)}, bf16[64,512]{1,0:T(8,128)(2,1)S(1)}, ...), condition=%wide.region_20.23_spmd, body=%wide.region_17.22_spmd.sunk | while | flops 17199112 | bytes 1253674 | solution.py:69
  30.4 3.8 %while.51 = (s32[]{:T(128)}, f32[32,1024]{1,0:T(8,128)S(1)}, bf16[128,1024]{1,0:T(8,128)(2,1)S(1)}, f32[32,128]{1,0:T(8,128)S(1)}, s32[]{:T(128)}, /*index=5*/s32[]{:T(128)}) while((s32[]{:T(128)}, f32[32,1024]{1,0:T(8,128)S(1)}, bf16[128,1024]{1,0:T(8,128)(2,1)S(1)}, f32[32,128]{1,0:T(8,128)S(1)}, s32[]{:T(128)}, ...), condition=%wide.region_19.21_spmd.clone, body=%wide.region_18.20_spmd.clone.sunk | while | flops 17129476 | bytes 1065039 | solution.py:40
  34.2 3.8 %while.51 = (s32[]{:T(128)}, f32[32,1024]{1,0:T(8,128)S(1)}, bf16[128,1024]{1,0:T(8,128)(2,1)S(1)}, f32[32,128]{1,0:T(8,128)S(1)}, s32[]{:T(128)}, /*index=5*/s32[]{:T(128)}) while((s32[]{:T(128)}, f32[32,1024]{1,0:T(8,128)S(1)}, bf16[128,1024]{1,0:T(8,128)(2,1)S(1)}, f32[32,128]{1,0:T(8,128)S(1)}, s32[]{:T(128)}, ...), condition=%wide.region_19.21_spmd.clone, body=%wide.region_18.20_spmd.clone.sunk | while | flops 17129476 | bytes 1065039 | solution.py:40
  38.1 0.7 %gather_fusion.1 = bf16[64,512]{1,0:T(8,128)(2,1)S(1)} fusion(bf16[64,512]{1,0:T(8,128)(2,1)S(1)} %get-tuple-element.133, s32[1024]{0:T(1024)S(1)} %pad_clamp_fusion.2), kind=kCustom, calls=%fused_computation.1.clone | custom fusion | bytes 131328 | tf_op jit(solution)/shard_map/jit(_take)/gather | solution.py:70
  38.8 0.7 %gather_fusion.3 = bf16[64,512]{1,0:T(8,128)(2,1)S(1)} fusion(bf16[64,512]{1,0:T(8,128)(2,1)S(1)} %get-tuple-element.134, s32[1024]{0:T(1024)S(1)} %pad_clamp_fusion), kind=kCustom, calls=%fused_computation.3.clone | custom fusion | bytes 131328 | tf_op jit(solution)/shard_map/jit(_take)/gather | solution.py:70
  39.6 0.6 %convolution_bitcast_fusion.1 = f32[2,1024,256]{2,1,0:T(8,128)S(1)} fusion(bf16[128,2,2,256]{3,0,1,2:T(8,128)(2,1)S(1)} %bitcast.87, bf16[64,64]{1,0:T(8,128)(2,1)S(1)} %get-tuple-element.236, bf16[64,64]{1,0:T(8,128)(2,1)S(1)} %get-tuple-element.237, bf16[64,64]{1,0:T(8,128)(2,1)S(1)} %get-tuple-element.238, bf16[64,512]{1,0:T(8,128)(2,1)S(1)} %get-tuple-element.232, ...), kind=kOutput, calls=%fused_computation.47 | convolution fusion | flops 152240128 | bytes 2473984 | tf_op jit(solution)/shard_map/ie,iap->aep/dot_general | solution.py:107
  40.7 0.6 %convolution_bitcast_fusion = f32[2,1024,256]{2,1,0:T(8,128)S(1)} fusion(bf16[128,2,2,256]{3,0,1,2:T(8,128)(2,1)S(1)} %bitcast.88, bf16[64,64]{1,0:T(8,128)(2,1)S(1)} %get-tuple-element.224, bf16[64,64]{1,0:T(8,128)(2,1)S(1)} %get-tuple-element.223, bf16[64,64]{1,0:T(8,128)(2,1)S(1)} %get-tuple-element.239, bf16[64,512]{1,0:T(8,128)(2,1)S(1)} %get-tuple-element.220, ...), kind=kOutput, calls=%fused_computation.46 | convolution fusion | flops 152240128 | bytes 2473984 | tf_op jit(solution)/shard_map/ie,iap->aep/dot_general | solution.py:107
  41.8 1.0 %copy.33 = bf16[2,2,512,256]{3,2,1,0:T(8,128)(2,1)} copy(bf16[2,2,512,256]{3,2,0,1:T(8,128)(2,1)S(1)} %pad_maximum_fusion) | data formatting | bytes 2097152 | tf_op jit(solution)/shard_map/stack | solution.py:137
  (164 shorter events, 17.6 us)
Async XLA Ops:
  0.0 17.6 %copy-start.1 = (s32[2,2,32]{2,1,0:T(2,128)S(1)}, s32[2,2,32]{2,1,0:T(2,128)}, u32[]{:S(2)}) copy-start(s32[2,2,32]{2,1,0:T(2,128)} %param.22) | copy-start | bytes 1540
  0.0 18.3 %copy-start = (bf16[2,2,64,64]{3,2,1,0:T(8,128)(2,1)S(1)}, bf16[2,2,64,64]{3,2,1,0:T(8,128)(2,1)}, u32[]{:S(2)}) copy-start(bf16[2,2,64,64]{3,2,1,0:T(8,128)(2,1)} %param.20) | copy-start | bytes 98308
  1.9 18.8 %all-to-all-start = ((bf16[2,1,8,16,2,256]{5,4,2,0,1,3:T(2,128)(2,1)}), bf16[2,1,8,16,2,256]{5,4,2,0,1,3:T(2,128)(2,1)S(1)}, u32[]{:S(2)}, u32[]{:S(2)}) async-start(bf16[2,1,8,16,2,256]{5,4,2,0,1,3:T(2,128)(2,1)} %bitcast.76), calls=%async_computation | async-start | bytes 524288 | tf_op jit(solution)/shard_map/all_to_all | solution.py:75
where the time goes:
time: 43.2 us; the launch traced here: 42.8 us
  matrix products  15 us (35%)
  local copies, waits for them, and re-layouts  9.99 us (23%)
  other arithmetic  8.13 us (19%)
  starting transfers between devices  5.38 us (12%)
  between operations  2.9 us (7%)
  loops' own time  1.45 us (3%)
    dot_general x32, matrix products, sweep(): jnp.dot(misfit, operator, preferred_element_type=jnp.float32)  12.6 us
    all_to_all x1, starting transfers between devices, shards(): lax.all_to_all(image_stack.reshape(halves, 1, acq_share, azb_all, range_l...  5.38 us
    unnamed x5, local copies, waits for them, and re-layouts  1.93 us
    another operation x5, other arithmetic  1.82 us
    scatter x2, local copies, waits for them, and re-layouts, pack_order(): jnp.zeros_like(lane_slot).at[lane_slot]  1.55 us
    reduce_sum x2, other arithmetic, pack_order(): live_total = jnp.sum(live_flags)  1.48 us
    gather x2, local copies, waits for them, and re-layouts, solve_lanes(): return jnp.take(result, lane_slot, axis=0)  1.4 us
    slice x1, local copies, waits for them, and re-layouts, shards(): range_group[column] - first_group  1.34 us
  transfers between devices with their start and end apart: 1, of which 0 were waited for; matrix products, arithmetic and copies ran while one was open for 25% of the time, Pallas kernels for 0%

commit v1 on v0

--- a/solution.py
+++ b/solution.py
@@ -72,13 +72,20 @@
 
 def shards(image_stack, steering, wiener_filter, range_group, lay_list, lay_count):
     halves, acq_share, azb_all, range_local, block_pixels = image_stack.shape
-    relaid = lax.all_to_all(
-        image_stack.reshape(halves, 1, acq_share, azb_all, range_local, block_pixels),
-        ("az", "acq"),
-        split_axis=3,
-        concat_axis=1,
-        tiled=True,
-    )
+    shard = image_stack.reshape(halves, 1, acq_share, azb_all, range_local, block_pixels)
+    ways, here = (lax.axis_size(("az", "acq")), lax.axis_index(("az", "acq")))
+    width = shard.shape[3] // ways
+    lengths = list(shard.shape)
+    lengths[3] = width
+    height = lengths[1]
+    lengths[1] = height * ways
+    full = jnp.zeros(lengths, shard.dtype)
+    for mask in range(ways):
+        part = lax.dynamic_slice_in_dim(shard, (here ^ mask) * width, width, axis=3)
+        if mask:
+            part = lax.ppermute(part, ("az", "acq"), [(d, d ^ mask) for d in range(ways)])
+        full = lax.dynamic_update_slice_in_dim(full, part, (here ^ mask) * height, axis=1)
+    relaid = full
     blocks = lay_list.shape[0]
     pixels = relaid.reshape(2 * K, blocks, range_local, block_pixels)
     first_group = lax.axis_index("rg") * GRP_DEV

time: 43.2 us -> 48.3 us (1.12)
  starting transfers between devices: 5.38 us -> 8.75 us
  waiting for transfers between devices: 0.01 us -> 1.96 us
  local copies, waits for them, and re-layouts: 9.99 us -> 9.23 us
    ppermute x0 -> x7, starting transfers between devices: none -> 8.75 us  [shards(): lax.ppermute(part, ('az', 'acq'), [(d, d ^ mask) for d in range(ways)])]
    all_to_all x1 -> x0, starting transfers between devices: 5.38 us -> none  [shards(): lax.all_to_all(image_stack.reshape(halves, 1, acq_share, azb_all, range_l...]
    ppermute x0 -> x7, waiting for transfers between devices: none -> 1.96 us  [shards(): lax.ppermute(part, ('az', 'acq'), [(d, d ^ mask) for d in range(ways)])]
    unnamed x5 -> x11, local copies, waits for them, and re-layouts: 1.93 us -> 0.05 us
    another operation x2 -> x3, local copies, waits for them, and re-layouts: 0.01 us -> 1.12 us
    another operation x5 -> x6, other arithmetic: 1.82 us -> 1.91 us
  transfers between devices with their start and end apart: 1 -> 7, of which waited for: 0 -> 2; matrix products, arithmetic and copies ran while one was open for 25% -> 23% of each run, Pallas kernels for 0% -> 0%
where the time goes in v1:
time: 48.3 us; the launch traced here: 47.7 us
  matrix products  15.1 us (31%)
  local copies, waits for them, and re-layouts  9.23 us (19%)
  starting transfers between devices  8.75 us (18%)
  other arithmetic  8.22 us (17%)
  between operations  3.09 us (6%)
  waiting for transfers between devices  1.96 us (4%)
  loops' own time  1.42 us (3%)
    dot_general x32, matrix products, sweep(): jnp.dot(misfit, operator, preferred_element_type=jnp.float32)  12.6 us
    ppermute x7, starting transfers between devices, shards(): lax.ppermute(part, ('az', 'acq'), [(d, d ^ mask) for d in range(ways)])  8.75 us
    ppermute x7, waiting for transfers between devices, shards(): lax.ppermute(part, ('az', 'acq'), [(d, d ^ mask) for d in range(ways)])  1.96 us
    another operation x6, other arithmetic  1.91 us
    scatter x2, local copies, waits for them, and re-layouts, pack_order(): jnp.zeros_like(lane_slot).at[lane_slot]  1.55 us
    reduce_sum x2, other arithmetic, pack_order(): live_total = jnp.sum(live_flags)  1.48 us
    gather x2, local copies, waits for them, and re-layouts, solve_lanes(): return jnp.take(result, lane_slot, axis=0)  1.4 us
    dot_general x2, matrix products, shards(): jnp.einsum('ie,iap->aep', operator, filtered, preferred_element_type=jnp....  1.34 us
  transfers between devices with their start and end apart: 7, of which 2 were waited for; matrix products, arithmetic and copies ran while one was open for 23% of the time, Pallas kernels for 0%

profile of v1, /device:TPU:27, one launch (start us, length us, event | category | flops | bytes accessed | tf_op | source)
XLA Modules:
  0.0 47.7 jit_solution(13416366937161482213)
XLA Ops:
  0.0 1.1 %constant_dynamic-slice_fusion = (bf16[2,8,2,2,256]{4,3,2,1,0:T(2,128)(2,1)S(1)}, bf16[2,8,2,2,256]{4,3,2,1,0:T(2,128)(2,1)S(1)}, bf16[2,8,2,2,256]{4,3,2,1,0:T(...) fusion(bf16[2,8,16,2,256]{4,3,2,1,0:T(2,128)(2,1)} %param.18, ...), kind=kLoop, calls=%fused_computation.143 | loop fusion | bytes 524320 | tf_op jit(solution)/shard_map/dynamic-slice.7
  1.1 0.7 %collective-permute-start = (bf16[2,1,8,2,2,256]{5,2,4,3,1,0:T(8,128)(2,1)S(1)}, bf16[2,1,8,2,2,256]{5,2,4,3,1,0:T(8,128)(2,1)S(1)}, u32[]{:S(2)}, u32[]{:S(2)}) collective-permute-start(bf16[2,1,8,2,2,256]{5,2,4,3,1,0:T(8,128)(2,1)S(1)} %bitcast.115), channel_id=1, source_target_pairs={{0,1},{1,0},{4,5},{5,4},{8,9},{9,8},{12,13},{13,12},{2,3},{3,2},{6... | collective-permute-start | bytes 98312 | tf_op jit(solution)/shard_map/ppermute | solution.py:86
  2.1 1.5 %collective-permute-start.2 = (bf16[2,1,8,2,2,256]{5,2,4,3,1,0:T(8,128)(2,1)S(1)}, bf16[2,1,8,2,2,256]{5,2,4,3,1,0:T(8,128)(2,1)S(1)}, u32[]{:S(2)}, u32[]{:S(2)}) collective-permute-start(bf16[2,1,8,2,2,256]{5,2,4,3,1,0:T(8,128)(2,1)S(1)} %bitcast.113), channel_id=1, source_target_pairs={{0,5},{1,4},{4,1},{5,0},{8,13},{9,12},{12,9},{13,8},{2,7},{3,6},{6... | collective-permute-start | bytes 98312 | tf_op jit(solution)/shard_map/ppermute | solution.py:86
  3.7 2.6 %collective-permute-start.4 = (bf16[2,1,8,2,2,256]{5,2,4,3,1,0:T(8,128)(2,1)S(1)}, bf16[2,1,8,2,2,256]{5,2,4,3,1,0:T(8,128)(2,1)S(1)}, u32[]{:S(2)}, u32[]{:S(2)}) collective-permute-start(bf16[2,1,8,2,2,256]{5,2,4,3,1,0:T(8,128)(2,1)S(1)} %bitcast.111), channel_id=1, source_target_pairs={{0,9},{1,8},{4,13},{5,12},{8,1},{9,0},{12,5},{13,4},{2,11},{3,10},... | collective-permute-start | bytes 98312 | tf_op jit(solution)/shard_map/ppermute | solution.py:86
  6.3 1.0 %slice_reduce_fusion.1 = (s32[2]{0:T(128)S(1)}, s32[2]{0:T(128)S(1)}) fusion(s32[2,2]{1,0:T(2,128)} %param.23), kind=kLoop, calls=%fused_computation.165 | loop fusion | bytes 32 | tf_op jit(solution)/shard_map/slice | solution.py:117
  7.3 0.7 %convert_reduce_fusion.2 = s32[]{:T(128)} fusion(s32[2]{0:T(128)S(1)} %get-tuple-element.176), kind=kLoop, calls=%fused_computation.159 | loop fusion | flops 191 | bytes 12 | tf_op jit(solution)/shard_map/reduce_sum | solution.py:46
  8.4 0.8 %convert_reduce_fusion.3 = s32[]{:T(128)} fusion(s32[2]{0:T(128)S(1)} %get-tuple-element.175), kind=kLoop, calls=%fused_computation.162 | loop fusion | flops 191 | bytes 12 | tf_op jit(solution)/shard_map/reduce_sum | solution.py:46
  9.3 1.3 %fusion.95 = (s32[1]{0:T(128)}, s32[1]{0:T(128)}) fusion(s32[2]{0:T(128)} %param.21), kind=kLoop, calls=%fused_computation.182 | loop fusion | bytes 16 | tf_op jit(solution)/shard_map/slice | solution.py:98
  11.9 1.1 %select_reduce_fusion.1 = (bf16[2,64,512]{2,1,0:T(8,128)(2,1)S(1)}, bf16[2,64,512]{2,1,0:T(8,128)(2,1)S(1)}) fusion(bf16[2,2,64,512]{3,2,1,0:T(8,128)(2,1)} %param.19, pred[2]{0:T(512)(128)(4,1)S(1)} %iota_compare_fusion.5, pred[2]{0:T(512)(128)(4,1)S(1)} %iota_compare_fusion.4), kind=kLoop, calls=%fused_computation.70 | loop fusion | flops 393216 | bytes 524292 | tf_op jit(solution)/shard_map/reduce_sum | solution.py:99
  13.7 0.7 %fusion.93 = (s32[64]{0:T(128)S(1)}, s32[64]{0:T(128)S(1)}, s32[64]{0:T(128)S(1)}) fusion(s32[64,1]{1,0:T(8,128)S(1)} %reduce-window.16, pred[64,1]{1,0:T(8,128)(4,1)S(1)} %lt.225, s32[64,1]{1,0:T(8,128)S(1)} %reduce-window.19, s32[]{:T(128)} %convert_reduce_fusion.2), kind=kLoop, calls=%fused_computation.180 | loop fusion | flops 576 | bytes 1348 | tf_op jit(solution)/shard_map/reduce-window.2
  14.4 0.8 %scatter_custom_fusion.1 = s32[64]{0:T(128)S(1)} fusion(s32[64]{0:T(128)S(1)} %get-tuple-element.173, s32[64]{0:T(128)S(1)} %iota.37, s32[]{:T(128)} %constant.143.clone.1), kind=kCustom, calls=%fused_computation.169 | custom fusion | bytes 260 | tf_op jit(solution)/shard_map/scatter | solution.py:51
  15.2 0.8 %fusion.92 = (s32[64]{0:T(128)S(1)}, s32[64]{0:T(128)S(1)}, s32[64]{0:T(128)S(1)}) fusion(s32[64,1]{1,0:T(8,128)S(1)} %reduce-window.14, pred[64,1]{1,0:T(8,128)(4,1)S(1)} %lt.224, s32[64,1]{1,0:T(8,128)S(1)} %reduce-window.15, s32[]{:T(128)} %convert_reduce_fusion.3), kind=kLoop, calls=%fused_computation.179 | loop fusion | flops 576 | bytes 1348 | tf_op jit(solution)/shard_map/reduce-window
  16.0 0.8 %scatter_custom_fusion = s32[64]{0:T(128)S(1)} fusion(s32[64]{0:T(128)S(1)} %get-tuple-element.170, s32[64]{0:T(128)S(1)} %iota.35, s32[]{:T(128)} %constant.143.clone.1), kind=kCustom, calls=%fused_computation.171 | custom fusion | bytes 260 | tf_op jit(solution)/shard_map/scatter | solution.py:51
  20.0 3.5 %collective-permute-start.6 = (bf16[2,1,8,2,2,256]{5,2,4,3,1,0:T(8,128)(2,1)S(1)}, bf16[2,1,8,2,2,256]{5,2,4,3,1,0:T(8,128)(2,1)S(1)}, u32[]{:S(2)}, u32[]{:S(2)}) collective-permute-start(bf16[2,1,8,2,2,256]{5,2,4,3,1,0:T(8,128)(2,1)S(1)} %bitcast.116), channel_id=1, source_target_pairs={{0,13},{1,12},{4,9},{5,8},{8,5},{9,4},{12,1},{13,0},{2,15},{3,14},... | collective-permute-start | bytes 98312 | tf_op jit(solution)/shard_map/ppermute | solution.py:86
  23.6 0.9 %collective-permute-done.5 = bf16[2,1,8,2,2,256]{5,2,4,3,1,0:T(8,128)(2,1)S(1)} collective-permute-done((bf16[2,1,8,2,2,256]{5,2,4,3,1,0:T(8,128)(2,1)S(1)}, bf16[2,1,8,2,2,256]{5,2,4,3,1,0:T(8,128)(2,1)S(1)}, u32[]{:S(2)}, u32[]{:S(2)}) %collective-permute-start.5) | collective-permute-done | bytes 32800 | tf_op jit(solution)/shard_map/ppermute | solution.py:86
  24.5 1.0 %collective-permute-done.6 = bf16[2,1,8,2,2,256]{5,2,4,3,1,0:T(8,128)(2,1)S(1)} collective-permute-done((bf16[2,1,8,2,2,256]{5,2,4,3,1,0:T(8,128)(2,1)S(1)}, bf16[2,1,8,2,2,256]{5,2,4,3,1,0:T(8,128)(2,1)S(1)}, u32[]{:S(2)}, u32[]{:S(2)}) %collective-permute-start.6) | collective-permute-done | bytes 32800 | tf_op jit(solution)/shard_map/ppermute | solution.py:86
  26.7 7.7 %while.49 = (s32[]{:T(128)}, bf16[64,512]{1,0:T(8,128)(2,1)S(1)}, s32[]{:T(128)}, bf16[64,128]{1,0:T(8,128)(2,1)S(1)}, bf16[128,1024]{1,0:T(8,128)(2,1)S(1)}, /*...) while((s32[]{:T(128)}, bf16[64,512]{1,0:T(8,128)(2,1)S(1)}, ...), condition=%wide.region_20.23_spmd, body=%wide.region_17.22_spmd.sunk | while | flops 17199112 | bytes 1253690 | solution.py:69
  26.8 3.8 %while.51 = (s32[]{:T(128)}, f32[32,1024]{1,0:T(8,128)S(1)}, bf16[128,1024]{1,0:T(8,128)(2,1)S(1)}, f32[32,128]{1,0:T(8,128)S(1)}, s32[]{:T(128)}, /*index=5*/s32[]{:T(128)}) while((s32[]{:T(128)}, f32[32,1024]{1,0:T(8,128)S(1)}, bf16[128,1024]{1,0:T(8,128)(2,1)S(1)}, f32[32,128]{1,0:T(8,128)S(1)}, s32[]{:T(128)}, ...), condition=%wide.region_19.21_spmd.clone, body=%wide.region_18.20_spmd.clone.sunk | while | flops 17129476 | bytes 1065047 | solution.py:40
  30.6 3.8 %while.51 = (s32[]{:T(128)}, f32[32,1024]{1,0:T(8,128)S(1)}, bf16[128,1024]{1,0:T(8,128)(2,1)S(1)}, f32[32,128]{1,0:T(8,128)S(1)}, s32[]{:T(128)}, /*index=5*/s32[]{:T(128)}) while((s32[]{:T(128)}, f32[32,1024]{1,0:T(8,128)S(1)}, bf16[128,1024]{1,0:T(8,128)(2,1)S(1)}, f32[32,128]{1,0:T(8,128)S(1)}, s32[]{:T(128)}, ...), condition=%wide.region_19.21_spmd.clone, body=%wide.region_18.20_spmd.clone.sunk | while | flops 17129476 | bytes 1065047 | solution.py:40
  35.2 7.7 %while.47 = (s32[]{:T(128)}, bf16[64,512]{1,0:T(8,128)(2,1)S(1)}, s32[]{:T(128)}, bf16[64,128]{1,0:T(8,128)(2,1)S(1)}, bf16[128,1024]{1,0:T(8,128)(2,1)S(1)}, /*...) while((s32[]{:T(128)}, bf16[64,512]{1,0:T(8,128)(2,1)S(1)}, ...), condition=%wide.region_9.11_spmd, body=%wide.region_6.10_spmd.sunk | while | flops 17199112 | bytes 1253690 | solution.py:69
  35.2 3.8 %while.50 = (s32[]{:T(128)}, f32[32,1024]{1,0:T(8,128)S(1)}, bf16[128,1024]{1,0:T(8,128)(2,1)S(1)}, f32[32,128]{1,0:T(8,128)S(1)}, s32[]{:T(128)}, /*index=5*/s32[]{:T(128)}) while((s32[]{:T(128)}, f32[32,1024]{1,0:T(8,128)S(1)}, bf16[128,1024]{1,0:T(8,128)(2,1)S(1)}, f32[32,128]{1,0:T(8,128)S(1)}, s32[]{:T(128)}, ...), condition=%wide.region_8.9_spmd.clone, body=%wide.region_7.8_spmd.clone.sunk | while | flops 17129476 | bytes 1065047 | solution.py:40
  39.1 3.8 %while.50 = (s32[]{:T(128)}, f32[32,1024]{1,0:T(8,128)S(1)}, bf16[128,1024]{1,0:T(8,128)(2,1)S(1)}, f32[32,128]{1,0:T(8,128)S(1)}, s32[]{:T(128)}, /*index=5*/s32[]{:T(128)}) while((s32[]{:T(128)}, f32[32,1024]{1,0:T(8,128)S(1)}, bf16[128,1024]{1,0:T(8,128)(2,1)S(1)}, f32[32,128]{1,0:T(8,128)S(1)}, s32[]{:T(128)}, ...), condition=%wide.region_8.9_spmd.clone, body=%wide.region_7.8_spmd.clone.sunk | while | flops 17129476 | bytes 1065047 | solution.py:40
  43.7 0.7 %gather_fusion.1 = bf16[64,512]{1,0:T(8,128)(2,1)S(1)} fusion(bf16[64,512]{1,0:T(8,128)(2,1)S(1)} %get-tuple-element.133, s32[1024]{0:T(1024)S(1)} %pad_clamp_fusion.2), kind=kCustom, calls=%fused_computation.1.clone | custom fusion | bytes 131328 | tf_op jit(solution)/shard_map/jit(_take)/gather | solution.py:70
  46.7 1.0 %copy.36 = bf16[2,2,512,256]{3,2,1,0:T(8,128)(2,1)} copy(bf16[2,2,512,256]{3,2,0,1:T(8,128)(2,1)S(1)} %pad_maximum_fusion) | data formatting | bytes 2097152 | tf_op jit(solution)/shard_map/stack | solution.py:144
  (189 shorter events, 22.0 us)
Async XLA Ops:
  0.0 13.1 %copy-start = (bf16[2,2,64,64]{3,2,1,0:T(8,128)(2,1)S(1)}, bf16[2,2,64,64]{3,2,1,0:T(8,128)(2,1)}, u32[]{:S(2)}) copy-start(bf16[2,2,64,64]{3,2,1,0:T(8,128)(2,1)} %param.20) | copy-start | bytes 98308
  0.0 13.3 %copy-start.1 = (s32[2,2,32]{2,1,0:T(2,128)S(1)}, s32[2,2,32]{2,1,0:T(2,128)}, u32[]{:S(2)}) copy-start(s32[2,2,32]{2,1,0:T(2,128)} %param.22) | copy-start | bytes 1540
  1.1 18.8 %collective-permute-start = (bf16[2,1,8,2,2,256]{5,2,4,3,1,0:T(8,128)(2,1)S(1)}, bf16[2,1,8,2,2,256]{5,2,4,3,1,0:T(8,128)(2,1)S(1)}, u32[]{:S(2)}, u32[]{:S(2)}) collective-permute-start(bf16[2,1,8,2,2,256]{5,2,4,3,1,0:T(8,128)(2,1)S(1)} %bitcast.115), channel_id=1, source_target_pairs={{0,1},{1,0},{4,5},{5,4},{8,9},{9,8},{12,13},{13,12},{2,3},{3,2},{6... | collective-permute-start | bytes 98312 | tf_op jit(solution)/shard_map/ppermute | solution.py:86
  1.9 18.1 %collective-permute-start.1 = (bf16[2,1,8,2,2,256]{5,2,4,3,1,0:T(8,128)(2,1)S(1)}, bf16[2,1,8,2,2,256]{5,2,4,3,1,0:T(8,128)(2,1)S(1)}, u32[]{:S(2)}, u32[]{:S(2)}) collective-permute-start(bf16[2,1,8,2,2,256]{5,2,4,3,1,0:T(8,128)(2,1)S(1)} %bitcast.114), channel_id=1, source_target_pairs={{0,4},{1,5},{4,0},{5,1},{8,12},{9,13},{12,8},{13,9},{2,6},{3,7},{6... | collective-permute-start | bytes 98312 | tf_op jit(solution)/shard_map/ppermute | solution.py:86
  2.1 21.5 %collective-permute-start.2 = (bf16[2,1,8,2,2,256]{5,2,4,3,1,0:T(8,128)(2,1)S(1)}, bf16[2,1,8,2,2,256]{5,2,4,3,1,0:T(8,128)(2,1)S(1)}, u32[]{:S(2)}, u32[]{:S(2)}) collective-permute-start(bf16[2,1,8,2,2,256]{5,2,4,3,1,0:T(8,128)(2,1)S(1)} %bitcast.113), channel_id=1, source_target_pairs={{0,5},{1,4},{4,1},{5,0},{8,13},{9,12},{12,9},{13,8},{2,7},{3,6},{6... | collective-permute-start | bytes 98312 | tf_op jit(solution)/shard_map/ppermute | solution.py:86
  3.6 20.0 %collective-permute-start.3 = (bf16[2,1,8,2,2,256]{5,2,4,3,1,0:T(8,128)(2,1)S(1)}, bf16[2,1,8,2,2,256]{5,2,4,3,1,0:T(8,128)(2,1)S(1)}, u32[]{:S(2)}, u32[]{:S(2)}) collective-permute-start(bf16[2,1,8,2,2,256]{5,2,4,3,1,0:T(8,128)(2,1)S(1)} %bitcast.112), channel_id=1, source_target_pairs={{0,8},{1,9},{4,12},{5,13},{8,0},{9,1},{12,4},{13,5},{2,10},{3,11},... | collective-permute-start | bytes 98312 | tf_op jit(solution)/shard_map/ppermute | solution.py:86
  3.7 19.9 %collective-permute-start.4 = (bf16[2,1,8,2,2,256]{5,2,4,3,1,0:T(8,128)(2,1)S(1)}, bf16[2,1,8,2,2,256]{5,2,4,3,1,0:T(8,128)(2,1)S(1)}, u32[]{:S(2)}, u32[]{:S(2)}) collective-permute-start(bf16[2,1,8,2,2,256]{5,2,4,3,1,0:T(8,128)(2,1)S(1)} %bitcast.111), channel_id=1, source_target_pairs={{0,9},{1,8},{4,13},{5,12},{8,1},{9,0},{12,5},{13,4},{2,11},{3,10},... | collective-permute-start | bytes 98312 | tf_op jit(solution)/shard_map/ppermute | solution.py:86
  19.9 4.6 %collective-permute-start.5 = (bf16[2,1,8,2,2,256]{5,2,4,3,1,0:T(8,128)(2,1)S(1)}, bf16[2,1,8,2,2,256]{5,2,4,3,1,0:T(8,128)(2,1)S(1)}, u32[]{:S(2)}, u32[]{:S(2)}) collective-permute-start(bf16[2,1,8,2,2,256]{5,2,4,3,1,0:T(8,128)(2,1)S(1)} %bitcast.117), channel_id=1, source_target_pairs={{0,12},{1,13},{4,8},{5,9},{8,4},{9,5},{12,0},{13,1},{2,14},{3,15},... | collective-permute-start | bytes 98312 | tf_op jit(solution)/shard_map/ppermute | solution.py:86
  20.0 5.6 %collective-permute-start.6 = (bf16[2,1,8,2,2,256]{5,2,4,3,1,0:T(8,128)(2,1)S(1)}, bf16[2,1,8,2,2,256]{5,2,4,3,1,0:T(8,128)(2,1)S(1)}, u32[]{:S(2)}, u32[]{:S(2)}) collective-permute-start(bf16[2,1,8,2,2,256]{5,2,4,3,1,0:T(8,128)(2,1)S(1)} %bitcast.116), channel_id=1, source_target_pairs={{0,13},{1,12},{4,9},{5,8},{8,5},{9,4},{12,1},{13,0},{2,15},{3,14},... | collective-permute-start | bytes 98312 | tf_op jit(solution)/shard_map/ppermute | solution.py:86
